TPU v7x, 32 devices: a whole 2x2x4 slice. The times are simulated.
32 devices in a mesh: blk: 8 (over y, x, core), grp: 4 (over z).
Axes of the slice: x: 2, y: 2, z: 4, core: 2. Of those that a mesh axis runs over, the one named last changes fastest.
Arguments:
- trial_vec: float32 [1536, 24], P(('blk', 'grp')), may hold values from -6 to 6
- resid_vec: float32 [1536, 24], P(('blk', 'grp')), may hold values from -6 to 6
- search_dir: float32 [1536, 24], P(('blk', 'grp')), may hold values from -6 to 6
- trial_img: float32 [1536, 24], P(('blk', 'grp')), may hold values from -12 to 12
- search_img: float32 [1536, 24], P(('blk', 'grp')), may hold values from -12 to 12
- dens_exch: bfloat16 [1536, 20480], P(('blk', 'grp')), may hold values from -0.15625 to 0.15625
- dens_direct: bfloat16 [1536, 20480], P(('blk', 'grp')), may hold values from -0.15625 to 0.15625
- screen_mat: bfloat16 [20480, 20480], P('grp', 'blk'), may hold values from -0.0390625 to 0.0390625
- coulomb: float32 [20480], replicated, may hold values from 0.2 to 2
- valence_energy: float32 [96], replicated, may hold values from -3 to -1
- conduct_energy: float32 [256], replicated, may hold values from 0.5 to 3
- valence_index: int32 [1536], P(('blk', 'grp')), may hold values from 0 to 95, as said below
- conduct_index: int32 [1536], P(('blk', 'grp')), may hold values from 0 to 255, as said below
- ritz_coef: float32 [72, 24], replicated, may hold values from -1.75 to 1.75
Outputs:
- next_trial: float32 [1536, 24], P(('blk', 'grp'))
- next_trial_img: float32 [1536, 24], P(('blk', 'grp'))
- next_search: float32 [1536, 24], P(('blk', 'grp'))
- next_search_img: float32 [1536, 24], P(('blk', 'grp'))
- gram_matrix: float32 [72, 72], replicated
Inputs may be any that keep to these rules, and one draw needn't show every extreme that they name: `valence_index`: no two pairs have both the same valence band and the same conduction band. `conduct_index`: no two pairs have both the same valence band and the same conduction band.
All inputs are finite; a program needn't handle non-finite values.
Results may differ from a plain program's by a relative error of at most 0.0034.
Values may be sent and summed in bfloat16 or wider, within the bound.
A program may use at most 64 MiB of HBM per device.

v0:
```python
import jax
import jax.numpy as jnp
from jax import lax
from jax.sharding import PartitionSpec as P


def inner_rows(left, right):
    return lax.dot_general(
        left, right, (((0,), (0,)), ((), ())), preferred_element_type=jnp.float32
    )


def exact_dot(left, right):
    return jnp.dot(left, right, precision=lax.Precision.HIGHEST)


def shards(
    trial_vec,
    resid_vec,
    search_dir,
    trial_img,
    search_img,
    dens_exch,
    dens_direct,
    screen_mat,
    coulomb,
    valence_energy,
    conduct_energy,
    valence_index,
    conduct_index,
    ritz_coef,
):
    excitons = resid_vec.shape[1]
    devices = lax.axis_size("blk") * lax.axis_size("grp")
    g_share = coulomb.shape[0] // devices
    flat_index = lax.axis_index("blk") * lax.axis_size("grp") + lax.axis_index("grp")
    own_coulomb = lax.dynamic_slice_in_dim(coulomb, flat_index * g_share, g_share, 0)
    valence_hot = (
        valence_index[:, None] == jnp.arange(valence_energy.shape[0], dtype=jnp.int32)[None, :]
    ).astype(jnp.float32)
    conduct_hot = (
        conduct_index[:, None] == jnp.arange(conduct_energy.shape[0], dtype=jnp.int32)[None, :]
    ).astype(jnp.float32)
    gap = exact_dot(conduct_hot, conduct_energy) - exact_dot(valence_hot, valence_energy)
    resid_half = resid_vec.astype(jnp.bfloat16)
    regrouped = lax.all_to_all(dens_exch, ("blk", "grp"), split_axis=1, concat_axis=0, tiled=True)
    every_resid = lax.all_gather(resid_half, ("blk", "grp"), axis=0, tiled=True)
    proj = inner_rows(regrouped, every_resid)
    weighted = (own_coulomb[:, None] * proj).astype(jnp.bfloat16)
    exch_term = lax.psum_scatter(
        jnp.dot(regrouped, weighted, preferred_element_type=jnp.float32),
        ("blk", "grp"),
        scatter_dimension=0,
        tiled=True,
    )
    block_cols = screen_mat.shape[1]
    seen_total = lax.psum(inner_rows(dens_direct, resid_half), ("blk", "grp"))
    seen = seen_total.astype(jnp.bfloat16)
    col_part = lax.dynamic_slice_in_dim(seen, lax.axis_index("blk") * block_cols, block_cols, 0)
    screen_part = jnp.dot(screen_mat, col_part, preferred_element_type=jnp.float32)
    screened = lax.psum(screen_part.astype(jnp.bfloat16), "blk")
    screened_all = lax.all_gather(screened, "grp", axis=0, tiled=True)
    direct_term = jnp.dot(dens_direct, screened_all, preferred_element_type=jnp.float32)
    resid_img = gap[:, None] * resid_vec + 2.0 * exch_term - direct_term
    basis = jnp.concatenate([trial_vec, resid_vec, search_dir], axis=1)
    images = jnp.concatenate([trial_img, resid_img, search_img], axis=1)
    local_gram = lax.dot_general(
        basis, images, (((0,), (0,)), ((), ())), precision=lax.Precision.HIGHEST
    )
    gram_matrix = lax.psum(local_gram, ("blk", "grp"))
    lower = ritz_coef[excitons:]
    next_trial = exact_dot(basis, ritz_coef)
    next_trial_img = exact_dot(images, ritz_coef)
    next_search = exact_dot(jnp.concatenate([resid_vec, search_dir], axis=1), lower)
    next_search_img = exact_dot(jnp.concatenate([resid_img, search_img], axis=1), lower)
    return (next_trial, next_trial_img, next_search, next_search_img, gram_matrix)


def solution(mesh):
    return jax.shard_map(
        shards,
        mesh=mesh,
        in_specs=(
            P(("blk", "grp"), None),
            P(("blk", "grp"), None),
            P(("blk", "grp"), None),
            P(("blk", "grp"), None),
            P(("blk", "grp"), None),
            P(("blk", "grp"), None),
            P(("blk", "grp"), None),
            P("grp", "blk"),
            P(),
            P(),
            P(),
            P(("blk", "grp")),
            P(("blk", "grp")),
            P(),
        ),
        out_specs=(
            P(("blk", "grp"), None),
            P(("blk", "grp"), None),
            P(("blk", "grp"), None),
            P(("blk", "grp"), None),
            P(),
        ),
        check_vma=False,
    )
```

profile of v0, /device:TPU:0, one launch (start us, length us, event | category | flops | bytes accessed | tf_op | source)
XLA Modules:
  0.0 329.6 jit_solution(13059465515049194300)
XLA Ops:
  8.0 0.0 copy-start
  8.0 3.1 copy.28
  11.1 0.0 copy-start.2
  11.1 7.4 %all-to-all-start = ((bf16[48,32,640]{2,0,1:T(8,128)(2,1)}), bf16[48,32,640]{2,0,1:T(8,128)(2,1)}, u32[]{:S(2)}, u32[]{:S(2)}) async-start(bf16[48,32,640]{2,0,1:T(8,128)(2,1)} %bitcast.42), calls=%async_computation | async-start | bytes 3932160 | tf_op jit(solution)/shard_map/all_to_all | solution.py:46
  18.6 0.0 all-reduce.3.cloned.1.call-start
  18.6 0.0 copy-done
  18.6 0.0 copy-done.2
  18.7 1.7 fusion.19
  20.4 77.5 %all-reduce.4 = bf16[20480,24]{0,1:T(8,128)(2,1)S(1)} all-reduce(f32[20480,24]{0,1:T(8,128)} %fusion.19), channel_id=1, replica_groups=mesh['blk'=8,'grp'=4] {'blk','grp'}, use_global_device_ids=true, to_apply=%region_1.0 | all-reduce | flops 491520 | bytes 2949120 | tf_op jit(solution)/shard_map/psum | solution.py:57
  97.9 0.0 copy-start.6
  97.9 0.0 copy-start.4
  97.9 0.0 copy-start.7
  98.0 0.0 copy-start.8
  98.0 0.0 copy-start.9
  98.0 0.0 copy-start.10
  98.0 0.0 copy-start.1
  98.0 12.7 %fusion = bf16[5120,24]{0,1:T(8,128)(2,1)} fusion(bf16[5120,2560]{1,0:T(8,128)(2,1)} %param.21, bf16[20480,24]{0,1:T(8,128)(2,1)S(1)} %all-reduce.4, s32[]{:T(128)S(6)} %select_n.7), kind=kOutput, calls=%fused_computation.1 | convolution fusion | flops 629268480 | bytes 26583044 | tf_op jit(solution)/shard_map/dot_general | solution.py:60
  110.7 0.0 all-reduce.3.cloned.1.call-update
  110.7 0.0 reduce-scatter.4.cloned.1.call-start
  110.8 0.0 copy-done.6
  110.8 65.3 %all-gather = bf16[32,48,24]{1,2,0:T(8,128)(2,1)S(1)} all-gather(bf16[1,48,24]{1,2,0:T(8,128)(2,1)S(1)} %get-tuple-element.5), channel_id=1, replica_groups=mesh['blk'=8,'grp'=4] {'blk','grp'}, dimensions={0}, use_global_device_ids=true | all-gather | bytes 76032 | tf_op jit(solution)/shard_map/all_gather | solution.py:47
  176.2 0.3 reshape.18
  176.4 0.8 dynamic_slice.6
  177.2 0.0 copy-done.4
  177.2 0.0 copy-done.7
  177.2 0.0 copy-done.8
  177.2 0.2 convolution_bitcast_fusion.2
  177.4 0.0 copy-done.9
  177.4 0.0 copy-done.10
  177.4 0.2 fusion.3
  177.7 0.0 copy-done.1
  177.7 0.8 fusion.7
  178.5 0.8 fusion.27
  179.2 0.0 all-to-all-done
  179.2 3.2 convolution_bitcast_fusion
  182.4 1.2 copy.24
  183.6 0.0 reduce-scatter.4.cloned.1.call-update
  183.6 0.0 copy-start.3
  183.6 0.0 copy-start.5
  183.6 0.0 all-reduce.3.cloned.1.call-done
  183.7 18.4 %all_gather.7 = bf16[20480,24]{0,1:T(8,128)(2,1)S(1)} all-gather(bf16[5120,24]{0,1:T(8,128)(2,1)} %all-reduce.3.cloned.1.call-done), channel_id=1, replica_groups=mesh['blk'=8,'grp'=4] {'grp'}, dimensions={0}, use_global_device_ids=true | all-gather | bytes 1228800 | tf_op jit(solution)/shard_map/all_gather | solution.py:62
  202.0 75.9 %reduce-scatter.4.cloned.1.call-done = f32[48,24]{1,0:T(8,128)} async-done(((f32[1536,24]{1,0:T(8,128)}), f32[48,24]{1,0:T(8,128)}) %reduce-scatter.4.cloned.1.call-update) | async-done | bytes 4624
  278.0 0.8 copy.25
  278.8 0.6 fusion.2
  279.4 0.0 copy-done.3
  279.4 0.8 fusion.11
  280.2 0.0 copy-done.5
  280.3 0.2 fusion.5
  280.5 0.8 fusion.6
  281.2 40.9 %psum.23 = f32[72,72]{1,0:T(8,128)} all-reduce(f32[72,72]{1,0:T(8,128)S(1)} %fusion.5), channel_id=1, replica_groups=mesh['blk'=8,'grp'=4] {'blk','grp'}, use_global_device_ids=true, to_apply=%region_3.0 | all-reduce | flops 5184 | bytes 41472 | tf_op jit(solution)/shard_map/psum | solution.py:70
  (4 shorter events, 0.0 us)
Async XLA Ops:
  8.0 10.6 %copy-start = (bf16[48,20480]{1,0:T(8,128)(2,1)S(1)}, bf16[48,20480]{1,0:T(8,128)(2,1)}, u32[]{:S(2)}) copy-start(bf16[48,20480]{1,0:T(8,128)(2,1)} %param.20) | copy-start | bytes 5898244
  11.1 7.5 %copy-start.2 = (f32[48,24]{0,1:T(8,128)S(1)}, f32[48,24]{0,1:T(8,128)}, u32[]{:S(2)}) copy-start(f32[48,24]{0,1:T(8,128)} %param.15) | copy-start | bytes 13828
  11.1 168.1 %all-to-all-start = ((bf16[48,32,640]{2,0,1:T(8,128)(2,1)}), bf16[48,32,640]{2,0,1:T(8,128)(2,1)}, u32[]{:S(2)}, u32[]{:S(2)}) async-start(bf16[48,32,640]{2,0,1:T(8,128)(2,1)} %bitcast.42), calls=%async_computation | async-start | bytes 3932160 | tf_op jit(solution)/shard_map/all_to_all | solution.py:46
  18.6 165.1 %all-reduce.3.cloned.1.call-start = ((), (), s32[]{:S(2)}) async-start(), calls=%async_computation.2 | async-start | bytes 491520 | tf_op jit(solution)/shard_map/psum | solution.py:61
  97.9 12.9 %copy-start.6 = (f32[48,24]{0,1:T(8,128)S(1)}, f32[48,24]{0,1:T(8,128)}, u32[]{:S(2)}) copy-start(f32[48,24]{0,1:T(8,128)} %param.14) | copy-start | bytes 13828
  97.9 79.3 %copy-start.4 = (f32[48,24]{0,1:T(8,128)S(1)}, f32[48,24]{0,1:T(8,128)}, u32[]{:S(2)}) copy-start(f32[48,24]{0,1:T(8,128)} %param.16) | copy-start | bytes 13828
  97.9 79.3 %copy-start.7 = (f32[256]{0:T(256)S(1)}, f32[256]{0:T(256)}, u32[]{:S(2)}) copy-start(f32[256]{0:T(256)} %param.24) | copy-start | bytes 3076
  98.0 79.3 %copy-start.8 = (s32[48]{0:T(128)S(1)}, s32[48]{0:T(128)}, u32[]{:S(2)}) copy-start(s32[48]{0:T(128)} %param.26) | copy-start | bytes 580
  98.0 79.5 %copy-start.9 = (s32[48]{0:T(128)S(1)}, s32[48]{0:T(128)}, u32[]{:S(2)}) copy-start(s32[48]{0:T(128)} %param.25) | copy-start | bytes 580
  98.0 79.5 %copy-start.10 = (f32[96]{0:T(128)S(1)}, f32[96]{0:T(128)}, u32[]{:S(2)}) copy-start(f32[96]{0:T(128)} %param.23) | copy-start | bytes 1156
  98.0 79.7 %copy-start.1 = (f32[72,24]{0,1:T(8,128)S(1)}, f32[72,24]{0,1:T(8,128)}, u32[]{:S(2)}) copy-start(f32[72,24]{0,1:T(8,128)} %param.27) | copy-start | bytes 20740
  110.7 167.3 %reduce-scatter.4.cloned.1.call-start = ((), (), s32[]{:S(2)}) async-start(), calls=%async_computation.3 | async-start | bytes 811008
  183.6 95.8 %copy-start.3 = (f32[48,24]{0,1:T(8,128)S(1)}, f32[48,24]{0,1:T(8,128)}, u32[]{:S(2)}) copy-start(f32[48,24]{0,1:T(8,128)} %param.18) | copy-start | bytes 13828
  183.6 96.6 %copy-start.5 = (f32[48,24]{0,1:T(8,128)S(1)}, f32[48,24]{0,1:T(8,128)}, u32[]{:S(2)}) copy-start(f32[48,24]{0,1:T(8,128)} %param.17) | copy-start | bytes 13828
Sparse Core Ops, SparseCore 0:
  110.8 51.7 all-reduce.2
Sparse Core Ops, SparseCore 1:
  183.7 94.2 reduce-scatter.3
where the time goes:
time: 330 us
  blocking collectives  202 us (61%)
  waiting for transfers between devices  76 us (23%)
  matrix products  22 us (7%)
  between operations  15.7 us (5%)
  starting transfers between devices  7.52 us (2%)
  local copies, waits for them, and re-layouts  6.24 us (2%)
    psum x1, blocking collectives, shards(): seen_total = lax.psum(inner_rows(dens_direct, resid_half), ('blk', 'grp'))  77.5 us
    unnamed x3, waiting for transfers between devices  76 us
    all_gather x1, blocking collectives, shards(): every_resid = lax.all_gather(resid_half, ('blk', 'grp'), axis=0, tiled=True)  65.3 us
    psum x1, blocking collectives, shards(): gram_matrix = lax.psum(local_gram, ('blk', 'grp'))  40.9 us
    all_gather x1, blocking collectives, shards(): screened_all = lax.all_gather(screened, 'grp', axis=0, tiled=True)  18.4 us
    dot_general x1, matrix products, shards(): jnp.dot(screen_mat, col_part, preferred_element_type=jnp.float32)  12.7 us
    all_to_all x1, starting transfers between devices, shards(): lax.all_to_all(dens_exch, ('blk', 'grp'), split_axis=1, concat_axis=0, ti...  7.44 us
  transfers between devices with their start and end apart: 3, of which 1 were waited for; matrix products, arithmetic and copies ran while one was open for 7% of the time, Pallas kernels for 0%

commit v1 on v0

v1 whole, which is shorter than its diff:
```python
import functools

import jax
import jax.numpy as jnp
from jax import lax
from jax.experimental import pallas as pl
from jax.experimental.pallas import tpu as pltpu
from jax.sharding import PartitionSpec as P

MESH = pl.DeviceIdType.MESH
F32 = jnp.float32
BF16 = jnp.bfloat16
LANES = 128


def dot_nt(left, right):
    return lax.dot_general(left, right, (((1,), (1,)), ((), ())), preferred_element_type=F32)


def exact(left, right):
    return jnp.dot(left, right, precision=lax.Precision.HIGHEST, preferred_element_type=F32)


def exact_nt(left, right):
    return lax.dot_general(
        left, right, (((1,), (1,)), ((), ())), precision=lax.Precision.HIGHEST,
        preferred_element_type=F32,
    )


def kernel(
    nb, ng, gp, cp,
    trial_vec, resid_vec, search_dir, trial_img, search_img,
    dens_exch, dens_direct, screen_mat, coulomb,
    valence_energy, conduct_energy, valence_index, conduct_index, ritz_coef,
    out_trial, out_trial_img, out_search, out_search_img, out_gram,
    dd, de, ww, pair_out, pair_in, plane_out, plane_in, own_sum, grp_out, grp_in,
    seen_in, seen, fe, fd, part_out, part_in,
    ga_in, ga_mid, gb_in, gb_mid, bas, img, fresh, coef, v_row, c_row,
    load_sem, w_sem, pair_sem, plane_sem, grp_sem, seen_sem, part_sem,
    fe_z, fe_p, fe_c, fd_z, fd_p, fd_c, ga_sem, ga2_sem, gb_sem, gb2_sem,
):
    b = lax.axis_index("blk")
    g = lax.axis_index("grp")
    chips = nb // 2
    c, k = b // 2, b % 2
    total_g = dens_exch.shape[1]
    bc = total_g // nb
    rows = screen_mat.shape[0]
    ne = resid_vec.shape[0]
    ne2 = 2 * ne
    partner = 2 * c + (1 - k)

    def blk_peer(j):
        return lax.rem(b + j, nb)

    def chip_peer(j):
        return lax.rem(c + j, chips)

    def grp_peer(j):
        return lax.rem(g + j, ng)

    def remote(src, dst, sem, idx, dev):
        return pltpu.make_async_remote_copy(
            src_ref=src, dst_ref=dst, send_sem=sem.at[0, idx], recv_sem=sem.at[1, idx],
            device_id=dev, device_id_type=MESH,
        )

    load_d = pltpu.make_async_copy(dens_direct, dd, load_sem.at[0])
    load_e = pltpu.make_async_copy(dens_exch, de, load_sem.at[1])
    load_d.start()
    load_e.start()
    w_loads = []
    for s in range(-(-rows // cp)):
        n = min(cp, rows - s * cp)
        w_loads.append(
            pltpu.make_async_copy(
                screen_mat.at[pl.ds(s * cp, n)], ww.at[s, pl.ds(0, n)], w_sem.at[s]
            )
        )

    barrier = pltpu.get_barrier_semaphore()
    for j in range(1, nb):
        pl.semaphore_signal(barrier, inc=1, device_id=(blk_peer(j), g), device_id_type=MESH)
    for j in range(1, ng):
        pl.semaphore_signal(barrier, inc=1, device_id=(b, grp_peer(j)), device_id_type=MESH)

    pairs = resid_vec.shape[1]
    for ref in (bas, img, fresh, coef, v_row, c_row):
        ref[...] = jnp.zeros_like(ref)
    bas[0:ne, 0:pairs] = trial_vec[...]
    bas[ne:ne2, 0:pairs] = resid_vec[...]
    bas[ne2 : ne2 + ne, 0:pairs] = search_dir[...]
    img[0:ne, 0:pairs] = trial_img[...]
    img[ne2 : ne2 + ne, 0:pairs] = search_img[...]
    coef[:, 0 : ritz_coef.shape[1]] = ritz_coef[...]
    v_row[:, 0 : valence_energy.shape[1]] = valence_energy[...]
    c_row[:, 0 : conduct_energy.shape[1]] = conduct_energy[...]
    resid_t = bas[ne:ne2, 0:pairs]
    half_t = resid_t.astype(BF16)

    def width(q, step, limit):
        return max(0, min(step, limit - q * step))

    def project(blk, q):
        n = width(q, gp, bc)
        off = pl.multiple_of(blk * bc + q * gp, LANES)
        d = jnp.dot(half_t, dd[:, pl.ds(off, n)], preferred_element_type=F32)
        e = jnp.dot(half_t, de[:, pl.ds(off, n)], preferred_element_type=F32)
        return n, jnp.concatenate([d, e], axis=0)

    load_d.wait()
    load_e.wait()
    for copy in w_loads:
        copy.start()
    pl.semaphore_wait(barrier, nb - 1 + ng - 1)

    started = []
    order = list(range(1, chips)) + [0]
    pair = {}
    for j in order:
        dest = chip_peer(j)
        for q in range(ng):
            if width(q, gp, bc):
                n, value = project(2 * dest + (1 - k), q)
                pair_out[j, q, :, pl.ds(0, n)] = value.astype(BF16)
        pair[j] = remote(pair_out.at[j], pair_in.at[j], pair_sem, j, (partner, g))
        pair[j].start()

    plane = {}
    for j in order:
        dest = chip_peer(j)
        pair[j].wait_recv()
        for q in range(ng):
            if width(q, gp, bc):
                n, value = project(2 * dest + k, q)
                value = value + pair_in[j, q, :, pl.ds(0, n)].astype(F32)
                if j:
                    plane_out[j, q, :, pl.ds(0, n)] = value.astype(BF16)
                else:
                    own_sum[q, :, pl.ds(0, n)] = value
        if j:
            plane[j] = remote(
                plane_out.at[j], plane_in.at[j], plane_sem, j, (2 * dest + k, g)
            )
            plane[j].start()

    nv, nc = v_row.shape[1], c_row.shape[1]
    v_hot = lax.broadcasted_iota(jnp.int32, (nv, pairs), 0) == valence_index[...]
    c_hot = lax.broadcasted_iota(jnp.int32, (nc, pairs), 0) == conduct_index[...]
    gap = exact(c_row[...], c_hot.astype(F32)) - exact(v_row[...], v_hot.astype(F32))
    base_t = gap * resid_t
    below = lax.broadcasted_iota(jnp.int32, bas.shape, 0) >= ne
    basis = bas[...]
    old_img = img[...]
    turn = coef[...]
    out_trial[...] = exact(turn, basis)[:, 0:pairs]
    out_search[...] = exact(turn, jnp.where(below, basis, 0.0))[:, 0:pairs]
    img_top = exact(turn, old_img)[:, 0:pairs]
    img_low = exact(turn, jnp.where(below, old_img, 0.0))[:, 0:pairs]
    ga_in[b, 0:ne, :] = exact_nt(old_img[0:ne], basis)
    ga_in[b, ne:ne2, :] = exact_nt(old_img[ne2 : ne2 + ne], basis)
    ga = {}
    for j in range(1, nb):
        ga[j] = remote(ga_in.at[b], ga_in.at[b], ga_sem, j, (blk_peer(j), g))

    for j in range(1, chips):
        plane[j].wait_recv()

    zsum = {}
    own_q = None
    def plane_total(q):
        value = own_sum[q]
        for j in range(1, chips):
            value = value + plane_in[j, q].astype(F32)
        return value

    for j in range(1, ng):
        q = grp_peer(j)
        grp_out[j] = plane_total(q).astype(BF16)
        zsum[j] = remote(grp_out.at[j], grp_in.at[j], grp_sem, j, (b, q))
        zsum[j].start()
    value = plane_total(g)
    for j in range(1, ng):
        zsum[j].wait_recv()
        value = value + grp_in[j].astype(F32)
    seen_in[g] = value[0:ne].astype(BF16)
    sz = {}
    for j in range(1, ng):
        sz[j] = remote(seen_in.at[g], seen_in.at[g], seen_sem, j, (b, grp_peer(j)))
        sz[j].start()
    c_off = b * bc + g * gp
    if ng * gp != bc:
        c_off = jnp.minimum(c_off, total_g - gp)
    fe[b, g] = (coulomb[:, pl.ds(pl.multiple_of(c_off, LANES), gp)] * value[ne:]).astype(BF16)

    def gather_grp(buf, sem):
        out = {}
        for j in range(1, ng):
            out[j] = remote(buf.at[b, g], buf.at[b, g], sem, j, (b, grp_peer(j)))
            out[j].start()
        return out

    def gather_chips(buf, sem, core_sem):
        out = {}
        for j in range(1, chips):
            out[j] = remote(buf.at[b], buf.at[b], sem, j, (2 * chip_peer(j) + k, g))
            out[j].start()
        core = {0: remote(buf.at[b], buf.at[b], core_sem, 0, (partner, g))}
        core[0].start()
        return out, core

    def from_chip(j):
        return 2 * lax.rem(c + chips - j, chips) + k

    def pass_on(buf, arrived, core, core_sem):
        for j in range(1, chips):
            arrived[j].wait_recv()
            src = from_chip(j)
            core[j] = remote(buf.at[src], buf.at[src], core_sem, j, (partner, g))
            core[j].start()

    ez = gather_grp(fe, fe_z)
    for copy in w_loads:
        copy.wait()
    for j in range(1, ng):
        sz[j].wait_recv()
    for q in range(ng):
        n = width(q, gp, bc)
        if n:
            seen[:, pl.ds(q * gp, n)] = seen_in[q, :, pl.ds(0, n)]

    seen_value = seen[...]
    parts = {}
    ep = ec = None
    for j in list(range(1, nb)) + [0]:
        dest = blk_peer(j)
        value = dot_nt(seen_value, ww[dest])
        if j:
            part_out[j] = value.astype(BF16)
            parts[j] = remote(part_out.at[j], part_in.at[j], part_sem, j, (dest, g))
            parts[j].start()
        if j == 1:
            for i in range(1, ng):
                ez[i].wait_recv()
            ep, ec = gather_chips(fe, fe_p, fe_c)
            for i in range(1, nb):
                ga[i].start()

    for j in range(1, nb):
        parts[j].wait_recv()
        value = value + part_in[j].astype(F32)
    fd[b, g] = value.astype(BF16)
    dz = gather_grp(fd, fd_z)

    def wait_all(copies):
        for copy in copies.values():
            copy.wait_recv()

    pass_on(fe, ep, ec, fe_c)
    wait_all(ga)
    for r in range(nb):
        ga_sum = ga_in[r] if r == 0 else ga_sum + ga_in[r]
    ga_mid[g] = ga_sum
    ga2 = {}
    for j in range(1, ng):
        ga2[j] = remote(ga_mid.at[g], ga_mid.at[g], ga2_sem, j, (b, grp_peer(j)))
        ga2[j].start()

    def exch_block(src, acc):
        for q in range(ng):
            n = width(q, gp, bc)
            if n:
                off = pl.multiple_of(src * bc + q * gp, LANES)
                acc = acc + dot_nt(fe[src, q, :, pl.ds(0, n)], de[:, pl.ds(off, n)])
        return acc

    def direct_block(src, acc):
        for q in range(ng):
            off = src * cp + q * rows
            if nb * cp != rows:
                off = jnp.minimum(off, total_g - cp)
            term = dot_nt(fd[src, q], dd[:, pl.ds(pl.multiple_of(off, LANES), cp)])
            if nb * cp != rows:
                term = jnp.where(src * cp < rows, term, 0.0)
            acc = acc + term
        return acc

    wait_all(dz)
    dp, dc = gather_chips(fd, fd_p, fd_c)

    acc = jnp.zeros((ne, pairs), F32)
    for j in range(chips):
        acc = exch_block(from_chip(j), acc)
    wait_all(ec)
    for j in range(chips):
        acc = exch_block(from_chip(j) + 1 - 2 * k, acc)
    acc_d = direct_block(b, jnp.zeros((ne, pairs), F32))
    dc[0].wait_recv()
    acc_d = direct_block(partner, acc_d)
    pass_on(fd, dp, dc, fd_c)
    for j in range(1, chips):
        acc_d = direct_block(from_chip(j), acc_d)
    for j in range(1, chips):
        dc[j].wait_recv()
        acc_d = direct_block(from_chip(j) + 1 - 2 * k, acc_d)

    img_t = base_t + 2.0 * acc - acc_d
    fresh[ne:ne2, 0:pairs] = img_t
    gb_in[b] = exact_nt(fresh[ne:ne2], basis)
    gb = {}
    for j in range(1, nb):
        gb[j] = remote(gb_in.at[b], gb_in.at[b], gb_sem, j, (blk_peer(j), g))
        gb[j].start()
    turned = exact(turn, fresh[...])[:, 0:pairs]
    out_search_img[...] = turned + img_low
    out_trial_img[...] = turned + img_top
    wait_all(ga2)
    for r in range(ng):
        ga_tot = ga_mid[r] if r == 0 else ga_tot + ga_mid[r]
    wait_all(gb)
    for r in range(nb):
        gb_sum = gb_in[r] if r == 0 else gb_sum + gb_in[r]
    gb_mid[g] = gb_sum
    gb2 = {}
    for j in range(1, ng):
        gb2[j] = remote(gb_mid.at[g], gb_mid.at[g], gb2_sem, j, (b, grp_peer(j)))
        gb2[j].start()
    wait_all(gb2)
    for r in range(ng):
        gb_tot = gb_mid[r] if r == 0 else gb_tot + gb_mid[r]
    gram_t = jnp.concatenate([ga_tot[0:ne], gb_tot, ga_tot[ne:]], axis=0)
    out_gram[...] = gram_t.T[0 : 3 * ne, :]

    for group in (pair, plane, zsum, sz, ez, ep, ec, parts, dz, dp, dc, ga, ga2, gb, gb2):
        for copy in group.values():
            copy.wait_send()


def up(size):
    return -(-size // LANES) * LANES


def shards(
    trial_vec, resid_vec, search_dir, trial_img, search_img, dens_exch, dens_direct,
    screen_mat, coulomb, valence_energy, conduct_energy, valence_index, conduct_index, ritz_coef,
):
    nb, ng = lax.axis_size("blk"), lax.axis_size("grp")
    pairs, ne = resid_vec.shape
    rows, bc = screen_mat.shape
    gp = -(-bc // (ng * LANES)) * LANES
    cp = -(-rows // (nb * LANES)) * LANES
    chips = nb // 2
    ne2 = 2 * ne
    total_g = dens_exch.shape[1]
    vmem = pl.BlockSpec(memory_space=pltpu.VMEM)
    hbm = pl.BlockSpec(memory_space=pl.ANY)
    sems = lambda n: pltpu.SemaphoreType.DMA((2, n))
    small = jax.ShapeDtypeStruct((ne, pairs), F32)
    side, wide = up(3 * ne), up(pairs)
    outs = pl.pallas_call(
        functools.partial(kernel, nb, ng, gp, cp),
        out_shape=(small, small, small, small, jax.ShapeDtypeStruct((3 * ne, 3 * ne), F32)),
        in_specs=[vmem] * 5 + [hbm] * 3 + [vmem] * 6,
        out_specs=(vmem,) * 5,
        scratch_shapes=[
            pltpu.VMEM((pairs, total_g), BF16),
            pltpu.VMEM((pairs, total_g), BF16),
            pltpu.VMEM((nb, cp, bc), BF16),
            pltpu.VMEM((chips, ng, ne2, gp), BF16),
            pltpu.VMEM((chips, ng, ne2, gp), BF16),
            pltpu.VMEM((chips, ng, ne2, gp), BF16),
            pltpu.VMEM((chips, ng, ne2, gp), BF16),
            pltpu.VMEM((ng, ne2, gp), F32),
            pltpu.VMEM((ng, ne2, gp), BF16),
            pltpu.VMEM((ng, ne2, gp), BF16),
            pltpu.VMEM((ng, ne, gp), BF16),
            pltpu.VMEM((ne, bc), BF16),
            pltpu.VMEM((nb, ng, ne, gp), BF16),
            pltpu.VMEM((nb, ng, ne, cp), BF16),
            pltpu.VMEM((nb, ne, cp), BF16),
            pltpu.VMEM((nb, ne, cp), BF16),
            pltpu.VMEM((nb, ne2, side), F32),
            pltpu.VMEM((ng, ne2, side), F32),
            pltpu.VMEM((nb, ne, side), F32),
            pltpu.VMEM((ng, ne, side), F32),
            pltpu.VMEM((side, wide), F32),
            pltpu.VMEM((side, wide), F32),
            pltpu.VMEM((side, wide), F32),
            pltpu.VMEM((ne, side), F32),
            pltpu.VMEM((1, up(valence_energy.shape[0])), F32),
            pltpu.VMEM((1, up(conduct_energy.shape[0])), F32),
            pltpu.SemaphoreType.DMA((2,)),
            pltpu.SemaphoreType.DMA((nb,)),
            sems(chips), sems(chips), sems(ng), sems(ng), sems(nb),
            sems(ng), sems(chips), sems(chips), sems(ng), sems(chips), sems(chips),
            sems(nb), sems(ng), sems(nb), sems(ng),
        ],
        compiler_params=pltpu.CompilerParams(
            collective_id=0, has_side_effects=True, vmem_limit_bytes=60 * 1024 * 1024
        ),
    )(
        trial_vec.T, resid_vec.T, search_dir.T, trial_img.T, search_img.T, dens_exch, dens_direct,
        screen_mat, coulomb[None, :], valence_energy[None, :], conduct_energy[None, :],
        valence_index[None, :], conduct_index[None, :], ritz_coef.T,
    )
    return tuple(x.T for x in outs[:4]) + (outs[4],)


def solution(mesh):
    rows = P(("blk", "grp"), None)
    return jax.shard_map(
        shards,
        mesh=mesh,
        in_specs=(rows,) * 7
        + (P("grp", "blk"), P(), P(), P(), P(("blk", "grp")), P(("blk", "grp")), P()),
        out_specs=(rows,) * 4 + (P(),),
        check_vma=False,
    )
```

time: 330 us -> 77 us (0.23)
  blocking collectives: 202 us -> 0 us
  waiting for transfers between devices: 76 us -> 0 us
  Pallas kernels: 0 us -> 69.2 us
  matrix products: 22 us -> 0 us
  between operations: 15.7 us -> 0.65 us
  starting transfers between devices: 7.52 us -> 0 us
    psum x2 -> x0, blocking collectives: 118 us -> none  [the longest x1 77.5 us: shards(): seen_total = lax.psum(inner_rows(dens_direct, resid_half), ('blk', 'grp'))]
    all_gather x2 -> x0, blocking collectives: 83.7 us -> none  [the longest x1 65.3 us: shards(): every_resid = lax.all_gather(resid_half, ('blk', 'grp'), axis=0, tiled=True)]
    unnamed x3 -> x0, waiting for transfers between devices: 76 us -> none
    pallas_call x0 -> x1, Pallas kernels: none -> 69.2 us  [shards(): pl.pallas_call(functools.partial(kernel, nb, ng, gp, cp), out_shape=(smal...]
    dot_general x11 -> x0, matrix products: 22 us -> none  [the longest x1 12.7 us: shards(): jnp.dot(screen_mat, col_part, preferred_element_type=jnp.float32)]
    all_to_all x1 -> x0, starting transfers between devices: 7.44 us -> none  [shards(): lax.all_to_all(dens_exch, ('blk', 'grp'), split_axis=1, concat_axis=0, ti...]
    unnamed x26 -> x5, local copies, waits for them, and re-layouts: 2.31 us -> 6.61 us
  transfers between devices with their start and end apart: 3 -> 0, of which waited for: 1 -> 0; matrix products, arithmetic and copies ran while one was open for 7% -> 0% of each run, Pallas kernels for 0% -> 0%
where the time goes in v1:
time: 77 us; the launch traced here: 76.5 us
  Pallas kernels  69.2 us (90%)
  local copies, waits for them, and re-layouts  6.61 us (9%)
    pallas_call x1, Pallas kernels, shards(): pl.pallas_call(functools.partial(kernel, nb, ng, gp, cp), out_shape=(smal...  69.2 us
    unnamed x5, local copies, waits for them, and re-layouts  6.61 us

profile of v1, /device:TPU:0, one launch (start us, length us, event | category | flops | bytes accessed | tf_op | source)
XLA Modules:
  0.0 76.5 jit_solution(12489132754871317948)
XLA Ops:
  0.6 69.2 %shard_map.173 = (f32[24,48]{1,0:T(8,128)}, f32[24,48]{1,0:T(8,128)}, f32[24,48]{1,0:T(8,128)}, f32[24,48]{1,0:T(8,128)}, f32[72,72]{1,0:T(8,128)}) custom-call(f32[24,48]{1,0:T(8,128)} %bitcast.16, f32[24,48]{1,0:T(8,128)} %bitcast.17, f32[24,48]{1,0:T(8,128)} %bitcast.18, f32[24,48]{1,0:T(8,128)} %bitcast.19, f32[24,48]{1,0:T(8,128)} %bitcast.20, ...), custom_call_target="tpu_custom_call" | custom-call | tf_op jit(solution)/shard_map/pallas_call | solution.py:361
  69.9 1.3 %copy.24 = f32[48,24]{0,1:T(8,128)} copy(f32[48,24]{0,1:T(8,128)} %bitcast.25) | data formatting | bytes 9216
  71.2 1.3 %copy.25 = f32[48,24]{0,1:T(8,128)} copy(f32[48,24]{0,1:T(8,128)} %bitcast.24) | data formatting | bytes 9216
  72.5 1.3 %copy.26 = f32[48,24]{0,1:T(8,128)} copy(f32[48,24]{0,1:T(8,128)} %bitcast.23) | data formatting | bytes 9216
  73.8 1.3 %copy.27 = f32[48,24]{0,1:T(8,128)} copy(f32[48,24]{0,1:T(8,128)} %bitcast.22) | data formatting | bytes 9216
  75.1 1.4 %copy.28 = f32[72,72]{1,0:T(8,128)} copy(f32[72,72]{1,0:T(8,128)} %get-tuple-element.24) | data formatting | bytes 41472

commit v2 on v1

--- a/solution.py
+++ b/solution.py
@@ -33,7 +33,7 @@
     trial_vec, resid_vec, search_dir, trial_img, search_img,
     dens_exch, dens_direct, screen_mat, coulomb,
     valence_energy, conduct_energy, valence_index, conduct_index, ritz_coef,
-    out_trial, out_trial_img, out_search, out_search_img, out_gram,
+    packed,
     dd, de, ww, pair_out, pair_in, plane_out, plane_in, own_sum, grp_out, grp_in,
     seen_in, seen, fe, fd, part_out, part_in,
     ga_in, ga_mid, gb_in, gb_mid, bas, img, fresh, coef, v_row, c_row,
@@ -154,8 +154,8 @@
     basis = bas[...]
     old_img = img[...]
     turn = coef[...]
-    out_trial[...] = exact(turn, basis)[:, 0:pairs]
-    out_search[...] = exact(turn, jnp.where(below, basis, 0.0))[:, 0:pairs]
+    packed[0 * ne : 1 * ne, 0:pairs] = exact(turn, basis)[:, 0:pairs]
+    packed[2 * ne : 3 * ne, 0:pairs] = exact(turn, jnp.where(below, basis, 0.0))[:, 0:pairs]
     img_top = exact(turn, old_img)[:, 0:pairs]
     img_low = exact(turn, jnp.where(below, old_img, 0.0))[:, 0:pairs]
     ga_in[b, 0:ne, :] = exact_nt(old_img[0:ne], basis)
@@ -235,7 +235,7 @@
     ep = ec = None
     for j in list(range(1, nb)) + [0]:
         dest = blk_peer(j)
-        value = dot_nt(seen_value, ww[dest])
+        value = dot_nt(ww[dest], seen_value).T
         if j:
             part_out[j] = value.astype(BF16)
             parts[j] = remote(part_out.at[j], part_in.at[j], part_sem, j, (dest, g))
@@ -252,6 +252,19 @@
         value = value + part_in[j].astype(F32)
     fd[b, g] = value.astype(BF16)
     dz = gather_grp(fd, fd_z)
+    dp, dc = {}, {}
+
+    def spread(z):
+        q = lax.rem(g + ng - z, ng)
+        for i in range(1, chips):
+            dp[i, z] = remote(
+                fd.at[b, q], fd.at[b, q], fd_p, i * ng + z, (2 * chip_peer(i) + k, g)
+            )
+            dp[i, z].start()
+        dc[0, z] = remote(fd.at[b, q], fd.at[b, q], fd_c, z, (partner, g))
+        dc[0, z].start()
+
+    spread(0)
 
     def wait_all(copies):
         for copy in copies.values():
@@ -275,19 +288,19 @@
                 acc = acc + dot_nt(fe[src, q, :, pl.ds(0, n)], de[:, pl.ds(off, n)])
         return acc
 
-    def direct_block(src, acc):
-        for q in range(ng):
-            off = src * cp + q * rows
-            if nb * cp != rows:
-                off = jnp.minimum(off, total_g - cp)
-            term = dot_nt(fd[src, q], dd[:, pl.ds(pl.multiple_of(off, LANES), cp)])
-            if nb * cp != rows:
-                term = jnp.where(src * cp < rows, term, 0.0)
-            acc = acc + term
-        return acc
-
-    wait_all(dz)
-    dp, dc = gather_chips(fd, fd_p, fd_c)
+    def direct_piece(src, z, acc):
+        q = lax.rem(g + ng - z, ng)
+        off = src * cp + q * rows
+        if nb * cp != rows:
+            off = jnp.minimum(off, total_g - cp)
+        term = dot_nt(fd[src, q], dd[:, pl.ds(pl.multiple_of(off, LANES), cp)])
+        if nb * cp != rows:
+            term = jnp.where(src * cp < rows, term, 0.0)
+        return acc + term
+
+    for z in range(1, ng):
+        dz[z].wait_recv()
+        spread(z)
 
     acc = jnp.zeros((ne, pairs), F32)
     for j in range(chips):
@@ -295,15 +308,21 @@
     wait_all(ec)
     for j in range(chips):
         acc = exch_block(from_chip(j) + 1 - 2 * k, acc)
-    acc_d = direct_block(b, jnp.zeros((ne, pairs), F32))
-    dc[0].wait_recv()
-    acc_d = direct_block(partner, acc_d)
-    pass_on(fd, dp, dc, fd_c)
-    for j in range(1, chips):
-        acc_d = direct_block(from_chip(j), acc_d)
-    for j in range(1, chips):
-        dc[j].wait_recv()
-        acc_d = direct_block(from_chip(j) + 1 - 2 * k, acc_d)
+    acc_d = jnp.zeros((ne, pairs), F32)
+    for z in range(ng):
+        for i in range(1, chips):
+            dp[i, z].wait_recv()
+            src = from_chip(i)
+            q = lax.rem(g + ng - z, ng)
+            dc[i, z] = remote(fd.at[src, q], fd.at[src, q], fd_c, i * ng + z, (partner, g))
+            dc[i, z].start()
+        for i in range(chips):
+            acc_d = direct_piece(from_chip(i), z, acc_d)
+    for z in range(ng):
+        for i in range(chips):
+            dc[i, z].wait_recv()
+        for i in range(chips):
+            acc_d = direct_piece(from_chip(i) + 1 - 2 * k, z, acc_d)
 
     img_t = base_t + 2.0 * acc - acc_d
     fresh[ne:ne2, 0:pairs] = img_t
@@ -313,8 +332,8 @@
         gb[j] = remote(gb_in.at[b], gb_in.at[b], gb_sem, j, (blk_peer(j), g))
         gb[j].start()
     turned = exact(turn, fresh[...])[:, 0:pairs]
-    out_search_img[...] = turned + img_low
-    out_trial_img[...] = turned + img_top
+    packed[3 * ne : 4 * ne, 0:pairs] = turned + img_low
+    packed[1 * ne : 2 * ne, 0:pairs] = turned + img_top
     wait_all(ga2)
     for r in range(ng):
         ga_tot = ga_mid[r] if r == 0 else ga_tot + ga_mid[r]
@@ -330,11 +349,19 @@
     for r in range(ng):
         gb_tot = gb_mid[r] if r == 0 else gb_tot + gb_mid[r]
     gram_t = jnp.concatenate([ga_tot[0:ne], gb_tot, ga_tot[ne:]], axis=0)
-    out_gram[...] = gram_t.T[0 : 3 * ne, :]
+    packed[4 * ne : 7 * ne, 0 : 3 * ne] = gram_t.T[0 : 3 * ne, :]
 
     for group in (pair, plane, zsum, sz, ez, ep, ec, parts, dz, dp, dc, ga, ga2, gb, gb2):
         for copy in group.values():
             copy.wait_send()
+
+
+def unpack(packed, *outs):
+    row = 0
+    for out in outs:
+        n, m = out.shape
+        out[...] = packed[row : row + n, 0:m]
+        row += n
 
 
 def up(size):
@@ -358,11 +385,11 @@
     sems = lambda n: pltpu.SemaphoreType.DMA((2, n))
     small = jax.ShapeDtypeStruct((ne, pairs), F32)
     side, wide = up(3 * ne), up(pairs)
-    outs = pl.pallas_call(
+    joined = pl.pallas_call(
         functools.partial(kernel, nb, ng, gp, cp),
-        out_shape=(small, small, small, small, jax.ShapeDtypeStruct((3 * ne, 3 * ne), F32)),
+        out_shape=jax.ShapeDtypeStruct((7 * ne, max(side, wide)), F32),
         in_specs=[vmem] * 5 + [hbm] * 3 + [vmem] * 6,
-        out_specs=(vmem,) * 5,
+        out_specs=vmem,
         scratch_shapes=[
             pltpu.VMEM((pairs, total_g), BF16),
             pltpu.VMEM((pairs, total_g), BF16),
@@ -393,7 +420,7 @@
             pltpu.SemaphoreType.DMA((2,)),
             pltpu.SemaphoreType.DMA((nb,)),
             sems(chips), sems(chips), sems(ng), sems(ng), sems(nb),
-            sems(ng), sems(chips), sems(chips), sems(ng), sems(chips), sems(chips),
+            sems(ng), sems(chips), sems(chips), sems(ng), sems(chips * ng), sems(chips * ng),
             sems(nb), sems(ng), sems(nb), sems(ng),
         ],
         compiler_params=pltpu.CompilerParams(
@@ -404,6 +431,12 @@
         screen_mat, coulomb[None, :], valence_energy[None, :], conduct_energy[None, :],
         valence_index[None, :], conduct_index[None, :], ritz_coef.T,
     )
+    outs = pl.pallas_call(
+        unpack,
+        out_shape=(small,) * 4 + (jax.ShapeDtypeStruct((3 * ne, 3 * ne), F32),),
+        in_specs=[vmem],
+        out_specs=(vmem,) * 5,
+    )(joined)
     return tuple(x.T for x in outs[:4]) + (outs[4],)
 
 

time: 77 us -> 73.5 us (0.955)
  local copies, waits for them, and re-layouts: 6.61 us -> 0 us
  Pallas kernels: 69.2 us -> 72.7 us
    unnamed x5 -> x0, local copies, waits for them, and re-layouts: 6.61 us -> none
    pallas_call x1 -> x2, Pallas kernels: 69.2 us -> 72.7 us  [the longest x1 71.1 us: shards(): pl.pallas_call(functools.partial(kernel, nb, ng, gp, cp), out_shape=jax.S...]
where the time goes in v2:
time: 73.5 us; the launch traced here: 73.3 us
  Pallas kernels  72.7 us (99%)
    pallas_call x1, Pallas kernels, shards(): pl.pallas_call(functools.partial(kernel, nb, ng, gp, cp), out_shape=jax.S...  71.1 us
    pallas_call x1, Pallas kernels, shards(): pl.pallas_call(unpack, out_shape=(small,) * 4 + (jax.ShapeDtypeStruct((3...  1.53 us

profile of v2, /device:TPU:0, one launch (start us, length us, event | category | flops | bytes accessed | tf_op | source)
XLA Modules:
  0.0 73.3 jit_solution(14410080132126276917)
XLA Ops:
  0.6 71.1 %shard_map.173.packed = f32[168,128]{1,0:T(8,128)} custom-call(f32[24,48]{1,0:T(8,128)} %bitcast.16, f32[24,48]{1,0:T(8,128)} %bitcast.17, f32[24,48]{1,0:T(8,128)} %bitcast.18, f32[24,48]{1,0:T(8,128)} %bitcast.19, f32[24,48]{1,0:T(8,128)} %bitcast.20, bf16[48,20480]{1,0:T(8,128)(2,1)} %dens_exch.1, bf16[48,20480]{1,0:T(8,128)(2,1)} %dens_direct.1, ...), custom_call_target="tpu_custom_call" | custom-call | tf_op jit(solution)/shard_map/pallas_call | solution.py:388
  71.8 1.5 %shard_map.174 = (f32[24,48]{1,0:T(8,128)}, f32[24,48]{1,0:T(8,128)}, f32[24,48]{1,0:T(8,128)}, f32[24,48]{1,0:T(8,128)}, f32[72,72]{1,0:T(8,128)}) custom-call(f32[168,128]{1,0:T(8,128)} %shard_map.173.packed), custom_call_target="tpu_custom_call" | custom-call | tf_op jit(solution)/shard_map/pallas_call | solution.py:434
